TPU v7x, 32 devices: a whole 2x2x4 slice. The times are simulated.
32 devices in a mesh: row: 4 (over z), col: 8 (over y, x, core).
Axes of the slice: x: 2, y: 2, z: 4, core: 2. Of those that a mesh axis runs over, the one named last changes fastest.
Arguments:
- query_grid: bfloat16 [64, 64, 6144], P('row', 'col'), may hold values from -6 to 6
- key_grid: bfloat16 [64, 64, 6144], P('row', 'col'), may hold values from -6 to 6
- value_grid: bfloat16 [64, 64, 6144], P('row', 'col'), may hold values from -6 to 6
- sink_keys: bfloat16 [8, 6144], replicated, may hold values from -9 to 9
- sink_values: bfloat16 [8, 6144], replicated, may hold values from -6 to 6
- grad_output: bfloat16 [64, 64, 6144], P('row', 'col'), may hold values from -6 to 6
- block_input: bfloat16 [64, 64, 6144], P('row', 'col'), may hold values from -6 to 6
- in_weight: bfloat16 [6144, 12288], P(None, 'col'), may hold values from -0.078125 to 0.078125
- in_bias: float32 [12288], P('col'), may hold values from -3 to 3
Outputs:
- attn_out: bfloat16 [64, 64, 6144], P('row', 'col')
- grad_query: bfloat16 [64, 64, 6144], P('row', 'col')
- grad_key: bfloat16 [64, 64, 6144], P('row', 'col')
- grad_value: bfloat16 [64, 64, 6144], P('row', 'col')
- grad_sink_keys: bfloat16 [8, 6144], replicated
- grad_sink_values: bfloat16 [8, 6144], replicated
- hidden: bfloat16 [64, 64, 12288], P('row', None, 'col')
All inputs are finite; a program needn't handle non-finite values.
Results may differ from a plain program's by a relative error of at most 0.017.
Values may be sent and summed in bfloat16 or wider, within the bound.
A program may use at most 192 MiB of HBM per device.

v0:
```python
import functools
import math

import jax
import jax.numpy as jnp
from jax import lax
from jax.experimental import pallas as pl
from jax.experimental.pallas import tpu as pltpu
from jax.sharding import PartitionSpec as P

HEAD_DIM = 128
WIN = 16
MESH = pl.DeviceIdType.MESH
F32 = jnp.float32
BF16 = jnp.bfloat16
CHUNKS = 12
GROUPS = 8
UNROLL = 2
AHEAD = 4
LAG = 2


def bits(r):
    return bin(r).count("1")


def parent(r, tree):
    if tree == 0:
        return r & ~(1 << (r.bit_length() - 1))
    return r & (r - 1)


def dot_nt(a, b):
    return lax.dot_general(a, b, (((1,), (1,)), ((), ())), preferred_element_type=F32)


def dot_nn(a, b):
    return lax.dot_general(a, b, (((1,), (0,)), ((), ())), preferred_element_type=F32)


def dot_tn(a, b):
    return lax.dot_general(a, b, (((0,), (0,)), ((), ())), preferred_element_type=F32)


def kernel(
    rows,
    cols,
    q_in,
    k_in,
    v_in,
    g_in,
    x_in,
    w_in,
    sk_in,
    sv_in,
    bias,
    ao_out,
    gq_out,
    gk_out,
    gv_out,
    gsk_out,
    gsv_out,
    hid_out,
    qb,
    kb,
    vb,
    gb,
    pk,
    pv,
    rk,
    rv,
    xg,
    wb,
    acc,
    hid,
    sg,
    ra,
    sb,
    rb,
    rc,
    fin,
    sk,
    sv,
    load_sem,
    w_sem,
    xs_sem,
    xr_sem,
    ps_sem,
    pr_sem,
    kvs_sem,
    kvr_sem,
    gs_sem,
    gr_sem,
    a_sem,
    b_send,
    b_recv,
    c_send,
    c_recv,
    d_send,
    d_recv,
    e_sem,
    out_sem,
):
    tokens, width = q_in.shape
    units = w_in.shape[1]
    regs = gsk_out.shape[0]
    chips = cols // 2
    levels = chips.bit_length() - 1
    heads = width // HEAD_DIM
    per_group = heads // GROUPS
    kc = width // CHUNKS
    gw = width // GROUPS
    rw = width // rows
    scale = 1.0 / math.sqrt(HEAD_DIM)

    my_row = lax.axis_index("row")
    my_col = lax.axis_index("col")
    parity = my_col % 2
    chip = my_col // 2
    peer = (my_row, my_col + 1 - 2 * parity)

    def flipped(value, mask):
        for b in range(levels):
            if mask >> b & 1:
                value = value + (1 << b) * (1 - 2 * ((value // (1 << b)) % 2))
        return value

    def chip_dev(r):
        return (my_row, flipped(chip, r) * 2 + parity)

    for pad, given in ((sk, sk_in), (sv, sv_in)):
        pad[...] = jnp.zeros_like(pad)
        pad[:regs, :] = given[...]

    def load(src, dst, s):
        return pltpu.make_async_copy(src, dst, load_sem.at[s])

    own_rows = pl.ds(pl.multiple_of(my_col * tokens, tokens), tokens)
    load(x_in, xg.at[own_rows, :], 4).start()
    for s, (src, dst) in enumerate(((q_in, qb), (k_in, kb), (v_in, vb), (g_in, gb))):
        load(src, dst, s).start()

    def w_copy(c):
        slot = c % 2
        return pltpu.make_async_copy(
            w_in.at[pl.ds(pl.multiple_of(c * kc, kc), kc), :], wb.at[slot], w_sem.at[slot]
        )

    w_copy(0).start()

    barrier = pltpu.get_barrier_semaphore()
    pl.semaphore_signal(barrier, inc=1, device_id=peer, device_id_type=MESH)
    for r in range(1, chips):
        pl.semaphore_signal(barrier, inc=1, device_id=chip_dev(r), device_id_type=MESH)

    def row_dev(d):
        return ((my_row + d) % rows, my_col)

    for d in range(1, rows):
        pl.semaphore_signal(barrier, inc=1, device_id=row_dev(d), device_id_type=MESH)
    pl.semaphore_wait(barrier, 1 + chips - 1 + rows - 1)

    def group_cols(t):
        return pl.ds(pl.multiple_of(t * gw, gw), gw)

    def kv_copy(t, which):
        src, dst = ((k_in, pk), (v_in, pv))[which]
        c = group_cols(t)
        return pltpu.make_async_remote_copy(
            src_ref=src.at[:, c],
            dst_ref=dst.at[:, c],
            send_sem=kvs_sem.at[t, which],
            recv_sem=kvr_sem.at[t, which],
            device_id=peer,
            device_id_type=MESH,
        )

    def grad_copy(t, which):
        src, dst = ((pk, rk), (pv, rv))[which]
        c = group_cols(t)
        return pltpu.make_async_remote_copy(
            src_ref=src.at[:, c],
            dst_ref=dst.at[:, c],
            send_sem=gs_sem.at[t, which],
            recv_sem=gr_sem.at[t, which],
            device_id=peer,
            device_id_type=MESH,
        )

    def piece(c, r):
        origin = flipped(chip, r) * 2 + parity
        return xg.at[
            pl.ds(pl.multiple_of(origin * tokens, tokens), tokens),
            pl.ds(pl.multiple_of(c * kc, kc), kc),
        ]

    def peer_piece(c, r):
        origin = flipped(chip, r) * 2 + 1 - parity
        return xg.at[
            pl.ds(pl.multiple_of(origin * tokens, tokens), tokens),
            pl.ds(pl.multiple_of(c * kc, kc), kc),
        ]

    def hop(c, r, tree):
        up = parent(r, tree)
        block = piece(c, up)
        return pltpu.make_async_remote_copy(
            src_ref=block,
            dst_ref=block,
            send_sem=xs_sem.at[c, r],
            recv_sem=xr_sem.at[c, r],
            device_id=chip_dev(up ^ r),
            device_id_type=MESH,
        )

    def hop_in(c, r):
        block = piece(c, r)
        return pltpu.make_async_remote_copy(
            src_ref=block,
            dst_ref=block,
            send_sem=xs_sem.at[c, r],
            recv_sem=xr_sem.at[c, r],
            device_id=chip_dev(1),
            device_id_type=MESH,
        )

    def share(c, r):
        block = piece(c, r)
        return pltpu.make_async_remote_copy(
            src_ref=block,
            dst_ref=block,
            send_sem=ps_sem.at[c, r],
            recv_sem=pr_sem.at[c, r],
            device_id=peer,
            device_id_type=MESH,
        )

    def share_in(c, r):
        block = peer_piece(c, r)
        return pltpu.make_async_remote_copy(
            src_ref=block,
            dst_ref=block,
            send_sem=ps_sem.at[c, r],
            recv_sem=pr_sem.at[c, r],
            device_id=peer,
            device_id_type=MESH,
        )

    def send_children(c, r):
        for tree in range(2):

            @pl.when(c % 2 == tree)
            def _():
                for kid in range(1, chips):
                    if parent(kid, tree) == r:
                        hop(c, kid, tree).start()

    def send_own(c):
        send_children(c, 0)
        share(c, 0).start()

    for t in range(2):
        for which in range(2):
            kv_copy(t, which).start()
    load(x_in, xg.at[own_rows, :], 4).wait()
    for c in range(AHEAD):
        send_own(c)
    for t in range(2, GROUPS):
        for which in range(2):
            kv_copy(t, which).start()
    for s, (src, dst) in enumerate(((q_in, qb), (k_in, kb), (v_in, vb), (g_in, gb))):
        load(src, dst, s).wait()

    lane = lax.broadcasted_iota(jnp.int32, (tokens, HEAD_DIM), 1)

    def attend(first):
        at = [
            pl.ds(pl.multiple_of((first + j) * HEAD_DIM, HEAD_DIM), HEAD_DIM)
            for j in range(UNROLL)
        ]
        blank = jnp.zeros((HEAD_DIM - sk.shape[0], HEAD_DIM), BF16)
        done = []
        for c in at:
            q = qb[:, c]
            g = gb[:, c]
            keys = jnp.concatenate([kb[:, c], pk[:, c], sk[:, c], blank], axis=0)
            values = jnp.concatenate([vb[:, c], pv[:, c], sv[:, c], blank], axis=0)
            s = dot_nt(q, keys) * scale
            sw = s[:, : 2 * tokens]
            ss = jnp.where(lane < regs, s[:, 2 * tokens :], -1e30)
            s = jnp.concatenate([sw, ss], axis=1)
            e = jnp.exp(s - jnp.max(s, axis=-1, keepdims=True))
            p = e * (1.0 / jnp.sum(e, axis=-1, keepdims=True))
            weight = p.astype(BF16)
            o = dot_nn(weight, values).astype(BF16)
            delta = jnp.sum(g.astype(F32) * o.astype(F32), axis=-1, keepdims=True)
            dp = dot_nt(g, values)
            ds = (p * (dp - delta) * scale).astype(BF16)
            dq = dot_nn(ds, keys).astype(BF16)
            dk = dot_tn(ds, q)
            dv = dot_tn(weight, g)
            done.append((o, dq, dk, dv))
        for c, (o, dq, dk, dv) in zip(at, done):
            gb[:, c] = o
            qb[:, c] = dq
            kb[:, c] = dk[:tokens].astype(BF16)
            pk[:, c] = dk[tokens : 2 * tokens].astype(BF16)
            vb[:, c] = dv[:tokens].astype(BF16)
            pv[:, c] = dv[tokens : 2 * tokens].astype(BF16)
            sg[0, :, c] = dk[2 * tokens : 2 * tokens + regs]
            sg[1, :, c] = dv[2 * tokens : 2 * tokens + regs]

    mt = min(512, cols * tokens)
    nt = 256
    m_tiles = cols * tokens // mt
    n_tiles = units // nt

    def multiply(c):
        slot = c % 2
        kcols = pl.ds(pl.multiple_of(c * kc, kc), kc)

        def tile(i, part):
            m, n = i // n_tiles, i % n_tiles
            mrows = pl.ds(pl.multiple_of(m * mt, mt), mt)
            ncols = pl.ds(pl.multiple_of(n * nt, nt), nt)
            prod = dot_nn(xg[mrows, kcols], wb[slot, :, ncols])
            if part == 0:
                acc[mrows, ncols] = prod + bias[:, ncols]
            elif part == 1:
                acc[mrows, ncols] += prod
            else:
                z = acc[mrows, ncols] + prod
                y = 0.5 * z * (1.0 + lax.erf(z * math.sqrt(0.5)))
                y = y.astype(BF16)
                per = mt // tokens
                for j in range(per):
                    hid[
                        :, pl.ds(pl.multiple_of((m * per + j) * (tokens // WIN), tokens // WIN), tokens // WIN), ncols
                    ] = y[j * tokens : (j + 1) * tokens].reshape(WIN, tokens // WIN, nt)

        for part, when in ((0, c == 0), (1, (c > 0) & (c < CHUNKS - 1)), (2, c == CHUNKS - 1)):

            @pl.when(when)
            def _():
                @pl.loop(0, m_tiles * n_tiles)
                def _(i):
                    tile(i, part)

    def a_copy():
        return pltpu.make_async_remote_copy(
            src_ref=sg.at[1 - parity],
            dst_ref=ra,
            send_sem=a_sem.at[0],
            recv_sem=a_sem.at[1],
            device_id=peer,
            device_id_type=MESH,
        )

    def row_cols(r):
        return pl.ds(pl.multiple_of(r * rw, rw), rw)

    def b_copy(d):
        to = (my_row + d) % rows
        return pltpu.make_async_remote_copy(
            src_ref=sb.at[:, row_cols(to)],
            dst_ref=rb.at[d],
            send_sem=b_send.at[d],
            recv_sem=b_recv.at[d],
            device_id=(to, my_col),
            device_id_type=MESH,
        )

    def c_copy(r, origin):
        return pltpu.make_async_remote_copy(
            src_ref=rc.at[origin],
            dst_ref=rc.at[origin],
            send_sem=c_send.at[r],
            recv_sem=c_recv.at[r],
            device_id=chip_dev(r),
            device_id_type=MESH,
        )

    def d_copy(d, origin):
        part = fin.at[parity, :, row_cols(origin)]
        return pltpu.make_async_remote_copy(
            src_ref=part,
            dst_ref=part,
            send_sem=d_send.at[d],
            recv_sem=d_recv.at[d],
            device_id=row_dev(d),
            device_id_type=MESH,
        )

    def e_copy(half):
        return pltpu.make_async_remote_copy(
            src_ref=fin.at[half],
            dst_ref=fin.at[half],
            send_sem=e_sem.at[0],
            recv_sem=e_sem.at[1],
            device_id=peer,
            device_id_type=MESH,
        )

    grads = ((gb, ao_out), (qb, gq_out), (kb, gk_out), (vb, gv_out))

    def out_copy(s):
        src, dst = grads[s]
        return pltpu.make_async_copy(src, dst, out_sem.at[s])

    def sink_copy(s):
        return pltpu.make_async_copy(fin.at[s], (gsk_out, gsv_out)[s], out_sem.at[4 + s])

    def finish_group(t):
        c = group_cols(t)
        for which, (own, other) in enumerate(((kb, rk), (vb, rv))):
            grad_copy(t, which).wait_recv()
            own[:, c] = (own[:, c].astype(F32) + other[:, c].astype(F32)).astype(BF16)

    @pl.loop(0, CHUNKS + LAG * (levels - 1) + 1)
    def _(i):
        @pl.when(i + AHEAD < CHUNKS)
        def _():
            send_own(i + AHEAD)

        @pl.when(i < GROUPS)
        def _():
            for which in range(2):
                kv_copy(i, which).wait_recv()

            @pl.loop(0, per_group // UNROLL)
            def _(j):
                attend(i * per_group + j * UNROLL)

            for which in range(2):
                grad_copy(i, which).start()

        @pl.when((i >= 1) & (i <= GROUPS))
        def _():
            finish_group(i - 1)

        @pl.when(i == GROUPS)
        def _():
            for s in range(4):
                out_copy(s).start()
            a_copy().start()

        @pl.when(i == GROUPS + 1)
        def _():
            a_copy().wait_recv()
            sb[...] = sg[parity] + ra[...]
            for d in range(1, rows):
                b_copy(d).start()

        @pl.when(i == GROUPS + 2)
        def _():
            total = sb[:, row_cols(my_row)]
            for d in range(1, rows):
                b_copy(d).wait_recv()
                total = total + rb[d]
            rc[chip] = total
            for r in range(1, chips):
                c_copy(r, chip).start()

        @pl.when(i == GROUPS + 3)
        def _():
            for r in range(1, chips):
                c_copy(r, flipped(chip, r)).wait_recv()
            total = rc[0]
            for r in range(1, chips):
                total = total + rc[r]
            fin[parity, :, row_cols(my_row)] = total.astype(BF16)
            for d in range(1, rows):
                d_copy(d, my_row).start()

        @pl.when(i == GROUPS + 4)
        def _():
            for d in range(1, rows):
                d_copy(d, (my_row + rows - d) % rows).wait_recv()
            e_copy(parity).start()

        @pl.when(i == GROUPS + 5)
        def _():
            e_copy(1 - parity).wait_recv()
            for s in range(2):
                sink_copy(s).start()

        for level in range(1, levels + 1):
            c = i - LAG * (level - 1)

            @pl.when((c >= 0) & (c < CHUNKS))
            def _():
                for r in range(1, chips):
                    if bits(r) == level:
                        hop_in(c, r).wait_recv()
                        send_children(c, r)
                        share(c, r).start()

        c = i - LAG * (levels - 1) - 1

        @pl.when(c >= 0)
        def _():
            @pl.when(c + 1 < CHUNKS)
            def _():
                w_copy(c + 1).start()

            w_copy(c).wait()
            for r in range(chips):
                share_in(c, r).wait_recv()
            multiply(c)

    hid_copy = pltpu.make_async_copy(hid, hid_out, out_sem.at[6])
    hid_copy.start()

    @pl.loop(0, CHUNKS)
    def _(c):
        for r in range(chips):
            share(c, r).wait_send()
        for r in range(1, chips):
            hop_in(c, r).wait_send()

    @pl.loop(0, GROUPS)
    def _(t):
        for which in range(2):
            kv_copy(t, which).wait_send()
            grad_copy(t, which).wait_send()

    a_copy().wait_send()
    for d in range(1, rows):
        b_copy(d).wait_send()
        d_copy(d, my_row).wait_send()
    for r in range(1, chips):
        c_copy(r, chip).wait_send()
    e_copy(parity).wait_send()
    for s in range(4):
        out_copy(s).wait()
    for s in range(2):
        sink_copy(s).wait()
    hid_copy.wait()


def local(
    rows,
    cols,
    query_grid,
    key_grid,
    value_grid,
    sink_keys,
    sink_values,
    grad_output,
    block_input,
    in_weight,
    in_bias,
):
    tile_rows, tile_cols, width = query_grid.shape
    tokens = tile_rows * tile_cols
    regs = sink_keys.shape[0]
    units = in_weight.shape[1]
    chips = cols // 2
    kc = width // CHUNKS
    rw = width // rows

    def flat(a):
        return a.reshape(tokens, width)

    hbm = pl.BlockSpec(memory_space=pl.ANY)
    vmem = pl.BlockSpec(memory_space=pltpu.VMEM)
    grid = jax.ShapeDtypeStruct((tokens, width), BF16)
    sink = jax.ShapeDtypeStruct((regs, width), BF16)
    dma = pltpu.SemaphoreType.DMA
    block = pltpu.VMEM((tokens, width), BF16)
    out = pl.pallas_call(
        functools.partial(kernel, rows, cols),
        out_shape=(
            grid,
            grid,
            grid,
            grid,
            sink,
            sink,
            jax.ShapeDtypeStruct((tile_rows, cols * tile_cols, units), BF16),
        ),
        in_specs=[hbm] * 6 + [vmem] * 3,
        out_specs=(hbm,) * 7,
        scratch_shapes=[block] * 8
        + [
            pltpu.VMEM((cols * tokens, width), BF16),
            pltpu.VMEM((2, kc, units), BF16),
            pltpu.VMEM((cols * tokens, units), F32),
            pltpu.VMEM((tile_rows, cols * tile_cols, units), BF16),
            pltpu.VMEM((2, regs, width), F32),
            pltpu.VMEM((regs, width), F32),
            pltpu.VMEM((regs, width), F32),
            pltpu.VMEM((rows, regs, rw), F32),
            pltpu.VMEM((chips, regs, rw), F32),
            pltpu.VMEM((2, regs, width), BF16),
            pltpu.VMEM((16, width), BF16),
            pltpu.VMEM((16, width), BF16),
            dma((5,)),
            dma((2,)),
            dma((CHUNKS, chips)),
            dma((CHUNKS, chips)),
            dma((CHUNKS, chips)),
            dma((CHUNKS, chips)),
            dma((GROUPS, 2)),
            dma((GROUPS, 2)),
            dma((GROUPS, 2)),
            dma((GROUPS, 2)),
            dma((2,)),
            dma((rows,)),
            dma((rows,)),
            dma((chips,)),
            dma((chips,)),
            dma((rows,)),
            dma((rows,)),
            dma((2,)),
            dma((7,)),
        ],
        compiler_params=pltpu.CompilerParams(
            collective_id=0, has_side_effects=True, vmem_limit_bytes=60 * 1024 * 1024
        ),
        name="block",
    )(
        flat(query_grid),
        flat(key_grid),
        flat(value_grid),
        flat(grad_output),
        flat(block_input),
        in_weight,
        sink_keys,
        sink_values,
        in_bias.reshape(1, units),
    )
    shaped = tuple(a.reshape(tile_rows, tile_cols, width) for a in out[:4])
    return shaped + out[4:]


def solution(mesh):
    placed = (
        P("row", "col", None),
        P("row", "col", None),
        P("row", "col", None),
        P(),
        P(),
        P("row", "col", None),
        P("row", "col", None),
        P(None, "col"),
        P("col"),
    )
    return jax.shard_map(
        functools.partial(local, mesh.shape["row"], mesh.shape["col"]),
        mesh=mesh,
        in_specs=placed,
        out_specs=(
            P("row", "col", None),
            P("row", "col", None),
            P("row", "col", None),
            P("row", "col", None),
            P(),
            P(),
            P("row", None, "col"),
        ),
        check_vma=False,
    )
```

profile of v0, /device:TPU:0, one launch (start us, length us, event | category | flops | bytes accessed | tf_op | source)
XLA Modules:
  0.0 113.1 jit_solution(11057129186131465983)
XLA Ops:
  0.6 1.3 %reshape.49.bias = f32[1,1536]{1,0:T(1,128)} reshape(f32[1536]{0:T(1024)} %param.17) | data formatting | bytes 12288 | tf_op jit(solution)/shard_map/reshape | solution.py:631
  1.9 100.2 %block.1 = (bf16[128,6144]{1,0:T(8,128)(2,1)}, bf16[128,6144]{1,0:T(8,128)(2,1)}, bf16[128,6144]{1,0:T(8,128)(2,1)}, bf16[128,6144]{1,0:T(8,128)(2,1)}, bf16[8,6...) custom-call(bf16[128,6144]{1,0:T(8,128)(2,1)} %bitcast.9, bf16[128,6144]{1,0:T(8,128)(2,1)} %bitcast.10, ...), custom_call_target="tpu_custom_call" | custom-call | tf_op jit(solution)/shard_map/block/pallas_call | solution.py:571
  102.1 0.0 copy-start.3
  102.1 2.8 %copy.23 = bf16[16,8,6144]{2,1,0:T(8,128)(2,1)} copy(bf16[16,8,6144]{2,1,0:T(8,128)(2,1)} %bitcast.17) | data formatting | bytes 3145728
  104.9 0.0 copy-done.3
  104.9 0.0 copy-start.2
  104.9 1.1 %copy.24 = bf16[16,8,6144]{2,1,0:T(8,128)(2,1)} copy(bf16[16,8,6144]{2,1,0:T(8,128)(2,1)S(1)} %bitcast.16) | data formatting | bytes 3145728
  106.1 0.8 copy-done.2
  106.9 0.0 copy-start.1
  106.9 0.0 copy-start.5
  106.9 1.1 %copy.25 = bf16[16,8,6144]{2,1,0:T(8,128)(2,1)} copy(bf16[16,8,6144]{2,1,0:T(8,128)(2,1)S(1)} %bitcast.15) | data formatting | bytes 3145728
  108.1 0.8 copy-done.1
  108.9 0.0 copy-start.4
  108.9 0.0 copy-start
  108.9 1.1 %copy.26 = bf16[16,8,6144]{2,1,0:T(8,128)(2,1)} copy(bf16[16,8,6144]{2,1,0:T(8,128)(2,1)S(1)} %bitcast.14) | data formatting | bytes 3145728
  110.0 0.0 copy-done.5
  110.0 0.6 copy.27
  110.7 0.0 copy-done.4
  110.7 0.6 copy.28
  111.3 0.1 copy-done
  111.4 1.7 %copy.29 = bf16[16,64,1536]{2,1,0:T(8,128)(2,1)} copy(bf16[16,64,1536]{2,1,0:T(8,128)(2,1)S(1)} %copy-done) | data formatting | bytes 6291456
Async XLA Ops:
  102.1 2.8 %copy-start.3 = (bf16[128,6144]{1,0:T(8,128)(2,1)S(1)}, bf16[128,6144]{1,0:T(8,128)(2,1)}, u32[]{:S(2)}) copy-start(bf16[128,6144]{1,0:T(8,128)(2,1)} %get-tuple-element.15) | copy-start | bytes 4718596
  104.9 2.0 %copy-start.2 = (bf16[128,6144]{1,0:T(8,128)(2,1)S(1)}, bf16[128,6144]{1,0:T(8,128)(2,1)}, u32[]{:S(2)}) copy-start(bf16[128,6144]{1,0:T(8,128)(2,1)} %get-tuple-element.16) | copy-start | bytes 4718596
  106.9 2.0 %copy-start.1 = (bf16[128,6144]{1,0:T(8,128)(2,1)S(1)}, bf16[128,6144]{1,0:T(8,128)(2,1)}, u32[]{:S(2)}) copy-start(bf16[128,6144]{1,0:T(8,128)(2,1)} %get-tuple-element.17) | copy-start | bytes 4718596
  106.9 3.1 %copy-start.5 = (bf16[8,6144]{1,0:T(8,128)(2,1)S(1)}, bf16[8,6144]{1,0:T(8,128)(2,1)}, u32[]{:S(2)}) copy-start(bf16[8,6144]{1,0:T(8,128)(2,1)} %get-tuple-element.32) | copy-start | bytes 294916
  108.9 1.8 %copy-start.4 = (bf16[8,6144]{1,0:T(8,128)(2,1)S(1)}, bf16[8,6144]{1,0:T(8,128)(2,1)}, u32[]{:S(2)}) copy-start(bf16[8,6144]{1,0:T(8,128)(2,1)} %get-tuple-element.33) | copy-start | bytes 294916
  108.9 2.5 %copy-start = (bf16[16,64,1536]{2,1,0:T(8,128)(2,1)S(1)}, bf16[16,64,1536]{2,1,0:T(8,128)(2,1)}, u32[]{:S(2)}) copy-start(bf16[16,64,1536]{2,1,0:T(8,128)(2,1)} %get-tuple-element.34) | copy-start | bytes 9437188
where the time goes:
time: 113 us
  Pallas kernels  100 us (88%)
  local copies, waits for them, and re-layouts  12.3 us (11%)
    pallas_call x1, Pallas kernels, local(): pl.pallas_call(functools.partial(kernel, rows, cols), out_shape=(grid, gr...  100 us
    unnamed x19, local copies, waits for them, and re-layouts  11 us

commit v1 on v0

v1 whole, which is shorter than its diff:
```python
import functools
import math

import jax
import jax.numpy as jnp
from jax import lax
from jax.experimental import pallas as pl
from jax.experimental.pallas import tpu as pltpu
from jax.sharding import PartitionSpec as P

HEAD_DIM = 128
WIN = 16
MESH = pl.DeviceIdType.MESH
F32 = jnp.float32
BF16 = jnp.bfloat16
CHUNKS = 12
GROUPS = 8
UNROLL = 2
NT = 512
PIECES = 6
WPARTS = 6
VMEM_LIMIT = 50 * 1024 * 1024


def bits(r):
    return bin(r).count("1")


def parent(r, tree):
    if tree == 0:
        return r & ~(1 << (r.bit_length() - 1))
    return r & (r - 1)


def dot_nt(a, b):
    return lax.dot_general(a, b, (((1,), (1,)), ((), ())), preferred_element_type=F32)


def dot_nn(a, b):
    return lax.dot_general(a, b, (((1,), (0,)), ((), ())), preferred_element_type=F32)


def dot_tn(a, b):
    return lax.dot_general(a, b, (((0,), (0,)), ((), ())), preferred_element_type=F32)


def kernel(
    rows,
    cols,
    q_in,
    k_in,
    v_in,
    g_in,
    x_in,
    w_in,
    sk_in,
    sv_in,
    bias,
    gb,
    qb,
    kb,
    vb,
    fin,
    hid,
    pk,
    pv,
    rk,
    rv,
    xg,
    wv,
    acc,
    sg,
    ra,
    sb,
    rb,
    rc,
    sk,
    sv,
    load_sem,
    w_sem,
    xs_sem,
    xr_sem,
    ps_sem,
    pr_sem,
    kvs_sem,
    kvr_sem,
    gs_sem,
    gr_sem,
    a_sem,
    b_send,
    b_recv,
    c_send,
    c_recv,
    d_send,
    d_recv,
    e_sem,
):
    tokens, width = q_in.shape
    units = w_in.shape[1]
    regs = fin.shape[1]
    chips = cols // 2
    levels = chips.bit_length() - 1
    last = chips - 1
    heads = width // HEAD_DIM
    per_group = heads // GROUPS
    kc = width // CHUNKS
    gw = width // GROUPS
    rw = width // rows
    wk = width // WPARTS
    pw = width // PIECES
    pair = 2 * tokens
    scale = 1.0 / math.sqrt(HEAD_DIM)
    nt = min(NT, units)
    n_tiles = units // nt

    my_row = lax.axis_index("row")
    my_col = lax.axis_index("col")
    parity = my_col % 2
    chip = my_col // 2
    peer = (my_row, my_col + 1 - 2 * parity)

    def flipped(value, mask):
        for b in range(levels):
            if mask >> b & 1:
                value = value + (1 << b) * (1 - 2 * ((value // (1 << b)) % 2))
        return value

    def chip_dev(r):
        return (my_row, flipped(chip, r) * 2 + parity)

    def row_dev(d):
        return ((my_row + d) % rows, my_col)

    def kids(r, tree):
        return [k for k in range(1, chips) if parent(k, tree) == r]

    def load(src, dst, s):
        return pltpu.make_async_copy(src, dst, load_sem.at[s])

    own_rows = pl.ds(pl.multiple_of(my_col * tokens, tokens), tokens)
    grads = ((q_in, qb), (k_in, kb), (v_in, vb), (g_in, gb))
    load(x_in, xg.at[own_rows, :], 4).start()
    for s, (src, dst) in enumerate(grads):
        load(src, dst, s).start()

    barrier = pltpu.get_barrier_semaphore()
    pl.semaphore_signal(barrier, inc=1, device_id=peer, device_id_type=MESH)
    for r in range(1, chips):
        pl.semaphore_signal(barrier, inc=1, device_id=chip_dev(r), device_id_type=MESH)
    for d in range(1, rows):
        pl.semaphore_signal(barrier, inc=1, device_id=row_dev(d), device_id_type=MESH)

    for pad, given in ((sk, sk_in), (sv, sv_in)):
        pad[...] = jnp.zeros_like(pad)
        pad[:regs, :] = given[...]

    pl.semaphore_wait(barrier, 1 + chips - 1 + rows - 1)

    def group_cols(t):
        return pl.ds(pl.multiple_of(t * gw, gw), gw)

    def kv_copy(t, which):
        src, dst = ((k_in, pk), (v_in, pv))[which]
        c = group_cols(t)
        return pltpu.make_async_remote_copy(
            src_ref=src.at[:, c],
            dst_ref=dst.at[:, c],
            send_sem=kvs_sem.at[t, which],
            recv_sem=kvr_sem.at[t, which],
            device_id=peer,
            device_id_type=MESH,
        )

    def grad_copy(t, which):
        src, dst = ((pk, rk), (pv, rv))[which]
        c = group_cols(t)
        return pltpu.make_async_remote_copy(
            src_ref=src.at[:, c],
            dst_ref=dst.at[:, c],
            send_sem=gs_sem.at[t, which],
            recv_sem=gr_sem.at[t, which],
            device_id=peer,
            device_id_type=MESH,
        )

    def piece(c, r, core):
        origin = flipped(chip, r) * 2 + core
        return xg.at[
            pl.ds(pl.multiple_of(origin * tokens, tokens), tokens),
            pl.ds(pl.multiple_of(c * kc, kc), kc),
        ]

    def hop(c, r, up):
        block = piece(c, up, parity)
        return pltpu.make_async_remote_copy(
            src_ref=block,
            dst_ref=block,
            send_sem=xs_sem.at[c, r],
            recv_sem=xr_sem.at[c, r],
            device_id=chip_dev(up ^ r),
            device_id_type=MESH,
        )

    def hop_in(c, r):
        block = piece(c, r, parity)
        return pltpu.make_async_remote_copy(
            src_ref=block,
            dst_ref=block,
            send_sem=xs_sem.at[c, r],
            recv_sem=xr_sem.at[c, r],
            device_id=chip_dev(1),
            device_id_type=MESH,
        )

    def share(c, r):
        block = piece(c, r, parity)
        return pltpu.make_async_remote_copy(
            src_ref=block,
            dst_ref=block,
            send_sem=ps_sem.at[c, r],
            recv_sem=pr_sem.at[c, r],
            device_id=peer,
            device_id_type=MESH,
        )

    def share_in(c, r):
        block = piece(c, r, 1 - parity)
        return pltpu.make_async_remote_copy(
            src_ref=block,
            dst_ref=block,
            send_sem=ps_sem.at[c, r],
            recv_sem=pr_sem.at[c, r],
            device_id=peer,
            device_id_type=MESH,
        )

    def w_copy(c):
        part = pl.ds(pl.multiple_of(c * wk, wk), wk)
        return pltpu.make_async_copy(w_in.at[part, :], wv.at[part, :], w_sem.at[c])

    firsts = [r for r in range(1, chips) if bits(r) == 1]

    def pass_on(j, r, tree):
        c = 2 * j + tree
        hop_in(c, r).wait_recv()
        for kid in kids(r, tree):
            hop(c, kid, r).start()
        share(c, r).start()

    def forward(j):
        for r in firsts:
            for tree in range(2):
                if kids(r, tree):
                    pass_on(j, r, tree)

    def settle(j):
        for r in firsts:
            for tree in range(2):
                if not kids(r, tree):
                    pass_on(j, r, tree)

    half = CHUNKS // 2

    for which in range(2):
        kv_copy(0, which).start()
    load(x_in, xg.at[own_rows, :], 4).wait()
    for leaf in range(2):

        @pl.loop(0, half)
        def _(j):
            for r in firsts:
                for tree in range(2):
                    if bool(kids(r, tree)) != bool(leaf):
                        hop(2 * j + tree, r, 0).start()

    @pl.loop(1, GROUPS)
    def _(t):
        for which in range(2):
            kv_copy(t, which).start()

    @pl.loop(0, CHUNKS)
    def _(c):
        share(c, 0).start()

    @pl.loop(0, WPARTS)
    def _(c):
        w_copy(c).start()

    for s, (src, dst) in enumerate(grads):
        load(src, dst, s).wait()

    lane = lax.broadcasted_iota(jnp.int32, (tokens, HEAD_DIM), 1)

    def attend(first):
        at = [
            pl.ds(pl.multiple_of((first + j) * HEAD_DIM, HEAD_DIM), HEAD_DIM)
            for j in range(UNROLL)
        ]
        blank = jnp.zeros((HEAD_DIM - sk.shape[0], HEAD_DIM), BF16)
        done = []
        for c in at:
            q = qb[:, c]
            g = gb[:, c]
            keys = jnp.concatenate([kb[:, c], pk[:, c], sk[:, c], blank], axis=0)
            values = jnp.concatenate([vb[:, c], pv[:, c], sv[:, c], blank], axis=0)
            s = dot_nt(q, keys) * scale
            sw = s[:, : 2 * tokens]
            ss = jnp.where(lane < regs, s[:, 2 * tokens :], -1e30)
            s = jnp.concatenate([sw, ss], axis=1)
            e = jnp.exp(s - jnp.max(s, axis=-1, keepdims=True))
            p = e * (1.0 / jnp.sum(e, axis=-1, keepdims=True))
            weight = p.astype(BF16)
            o = dot_nn(weight, values).astype(BF16)
            delta = jnp.sum(g.astype(F32) * o.astype(F32), axis=-1, keepdims=True)
            dp = dot_nt(g, values)
            ds = (p * (dp - delta) * scale).astype(BF16)
            dq = dot_nn(ds, keys).astype(BF16)
            dk = dot_tn(ds, q)
            dv = dot_tn(weight, g)
            done.append((o, dq, dk, dv))
        for c, (o, dq, dk, dv) in zip(at, done):
            gb[:, c] = o
            qb[:, c] = dq
            kb[:, c] = dk[:tokens].astype(BF16)
            pk[:, c] = dk[tokens : 2 * tokens].astype(BF16)
            vb[:, c] = dv[:tokens].astype(BF16)
            pv[:, c] = dv[tokens : 2 * tokens].astype(BF16)
            sg[0, :, c] = dk[2 * tokens : 2 * tokens + regs]
            sg[1, :, c] = dv[2 * tokens : 2 * tokens + regs]

    def rows_of(r):
        return pl.ds(pl.multiple_of(flipped(chip, r) * pair, pair), pair)

    def finish(z, r, ncols):
        y = 0.5 * z * (1.0 + lax.erf(z * math.sqrt(0.5)))
        y = y.astype(BF16)
        per = tokens // WIN
        first = flipped(chip, r) * (2 * per)
        for j in range(2):
            hid[:, pl.ds(pl.multiple_of(first + j * per, per), per), ncols] = y[
                j * tokens : (j + 1) * tokens
            ].reshape(WIN, per, nt)

    def tile_cols(n):
        return pl.ds(pl.multiple_of(n * nt, nt), nt)

    def whole_rows(r, n):
        ncols = tile_cols(n)
        z = dot_nn(xg[rows_of(r), :], wv[:, ncols]) + bias[ncols]
        finish(z, r, ncols)

    def a_copy():
        return pltpu.make_async_remote_copy(
            src_ref=sg.at[1 - parity],
            dst_ref=ra,
            send_sem=a_sem.at[0],
            recv_sem=a_sem.at[1],
            device_id=peer,
            device_id_type=MESH,
        )

    def row_cols(r):
        return pl.ds(pl.multiple_of(r * rw, rw), rw)

    def b_copy(d):
        to = (my_row + d) % rows
        return pltpu.make_async_remote_copy(
            src_ref=sb.at[:, row_cols(to)],
            dst_ref=rb.at[d],
            send_sem=b_send.at[d],
            recv_sem=b_recv.at[d],
            device_id=(to, my_col),
            device_id_type=MESH,
        )

    def c_copy(r, origin):
        return pltpu.make_async_remote_copy(
            src_ref=rc.at[origin],
            dst_ref=rc.at[origin],
            send_sem=c_send.at[r],
            recv_sem=c_recv.at[r],
            device_id=chip_dev(r),
            device_id_type=MESH,
        )

    def d_copy(d, origin):
        part = fin.at[parity, :, row_cols(origin)]
        return pltpu.make_async_remote_copy(
            src_ref=part,
            dst_ref=part,
            send_sem=d_send.at[d],
            recv_sem=d_recv.at[d],
            device_id=row_dev(d),
            device_id_type=MESH,
        )

    def e_copy(part):
        return pltpu.make_async_remote_copy(
            src_ref=fin.at[part],
            dst_ref=fin.at[part],
            send_sem=e_sem.at[0],
            recv_sem=e_sem.at[1],
            device_id=peer,
            device_id_type=MESH,
        )

    def finish_group(t):
        c = group_cols(t)
        for which, (own, other) in enumerate(((kb, rk), (vb, rv))):
            grad_copy(t, which).wait_recv()
            own[:, c] = (own[:, c].astype(F32) + other[:, c].astype(F32)).astype(BF16)

    def sinks_b():
        a_copy().wait_recv()
        sb[...] = sg[parity] + ra[...]
        for d in range(1, rows):
            b_copy(d).start()

    def sinks_c():
        total = sb[:, row_cols(my_row)]
        for d in range(1, rows):
            b_copy(d).wait_recv()
            total = total + rb[d]
        rc[chip] = total
        for r in range(1, chips):
            c_copy(r, chip).start()

    def sinks_d():
        for r in range(1, chips):
            c_copy(r, flipped(chip, r)).wait_recv()
        total = rc[0]
        for r in range(1, chips):
            total = total + rc[r]
        fin[parity, :, row_cols(my_row)] = total.astype(BF16)
        for d in range(1, rows):
            d_copy(d, my_row).start()

    def sinks_e():
        for d in range(1, rows):
            d_copy(d, (my_row + rows - d) % rows).wait_recv()
        e_copy(parity).start()

    @pl.loop(0, GROUPS + 1)
    def _(i):
        @pl.when(i < GROUPS)
        def _():
            for which in range(2):
                kv_copy(i, which).wait_recv()

            @pl.loop(0, per_group // UNROLL)
            def _(j):
                attend(i * per_group + j * UNROLL)

            for which in range(2):
                grad_copy(i, which).start()

        @pl.when(i >= 1)
        def _():
            finish_group(i - 1)

        @pl.when(i < half)
        def _():
            forward(i)

        @pl.when(i >= half)
        def _():
            settle(i - half)

    a_copy().start()

    @pl.loop(0, WPARTS)
    def _(c):
        w_copy(c).wait()

    @pl.loop(0, CHUNKS)
    def _(c):
        share_in(c, 0).wait_recv()

    done = GROUPS + 1 - half

    @pl.loop(0, n_tiles)
    def _(n):
        whole_rows(0, n)

        @pl.when(n == 0)
        def _():
            sinks_b()

        @pl.when(n + done < half)
        def _():
            settle(n + done)

    @pl.loop(min(half, n_tiles + done), half)
    def _(j):
        settle(j)

    sinks_c()

    for level in range(2, levels):

        @pl.loop(0, half)
        def _(j):
            for r in range(1, chips):
                if bits(r) == level:
                    for tree in range(2):
                        pass_on(j, r, tree)

    for r in sorted(range(1, last), key=bits):

        @pl.loop(0, CHUNKS)
        def _(c):
            share_in(c, r).wait_recv()

        @pl.loop(0, n_tiles)
        def _(n):
            whole_rows(r, n)

    def take(j):
        for c in range(CHUNKS // PIECES):
            c = j * (CHUNKS // PIECES) + c
            hop_in(c, last).wait_recv()
            share(c, last).start()

    def mix(j, n, part):
        kcols = pl.ds(pl.multiple_of(j * pw, pw), pw)
        ncols = tile_cols(n)
        z = dot_nn(xg[rows_of(last), kcols], wv[kcols, ncols])
        if part == 0:
            acc[:, ncols] = z + bias[ncols]
        elif part == 1:
            acc[:, ncols] += z
        else:
            finish(acc[:, ncols] + z, last, ncols)

    take(0)
    take(1)
    for part, (lo, hi) in enumerate(((0, 1), (1, PIECES - 1), (PIECES - 1, PIECES))):

        @pl.loop(lo, hi)
        def _(j):
            for c in range(CHUNKS // PIECES):
                share_in(j * (CHUNKS // PIECES) + c, last).wait_recv()

            @pl.loop(0, n_tiles)
            def _(n):
                mix(j, n, part)

            @pl.when(j + 2 < PIECES)
            def _():
                take(j + 2)

            @pl.when(j == PIECES - 2)
            def _():
                sinks_d()

    sinks_e()

    @pl.loop(0, CHUNKS)
    def _(c):
        for r in range(chips):
            share(c, r).wait_send()
        for r in range(1, chips):
            hop_in(c, r).wait_send()

    @pl.loop(0, GROUPS)
    def _(t):
        for which in range(2):
            kv_copy(t, which).wait_send()
            grad_copy(t, which).wait_send()

    a_copy().wait_send()
    for d in range(1, rows):
        b_copy(d).wait_send()
        d_copy(d, my_row).wait_send()
    for r in range(1, chips):
        c_copy(r, chip).wait_send()
    e_copy(1 - parity).wait_recv()
    e_copy(parity).wait_send()


def store(ao, gq, gk, gv, fin, hid, ao_out, gq_out, gk_out, gv_out, gsk_out, gsv_out, hid_out, sem):
    copies = [
        pltpu.make_async_copy(src, dst, sem.at[s])
        for s, (src, dst) in enumerate(
            (
                (hid, hid_out),
                (ao, ao_out),
                (gq, gq_out),
                (gk, gk_out),
                (gv, gv_out),
                (fin.at[0], gsk_out),
                (fin.at[1], gsv_out),
            )
        )
    ]
    for copy in copies:
        copy.start()
    for copy in copies:
        copy.wait()


def local(
    rows,
    cols,
    query_grid,
    key_grid,
    value_grid,
    sink_keys,
    sink_values,
    grad_output,
    block_input,
    in_weight,
    in_bias,
):
    tile_rows, tile_cols, width = query_grid.shape
    tokens = tile_rows * tile_cols
    regs = sink_keys.shape[0]
    units = in_weight.shape[1]
    chips = cols // 2
    rw = width // rows

    def flat(a):
        return a.reshape(tokens, width)

    hbm = pl.BlockSpec(memory_space=pl.ANY)
    vmem = pl.BlockSpec(memory_space=pltpu.VMEM)
    shapes = ((tokens, width),) * 4 + (
        (2, regs, width),
        (tile_rows, cols * tile_cols, units),
    )
    dma = pltpu.SemaphoreType.DMA
    block = pltpu.VMEM((tokens, width), BF16)
    held = pl.pallas_call(
        functools.partial(kernel, rows, cols),
        out_shape=tuple(pltpu.VMEM(shape, BF16) for shape in shapes),
        in_specs=[hbm] * 6 + [vmem] * 3,
        out_specs=(vmem,) * 6,
        scratch_shapes=[block] * 4
        + [
            pltpu.VMEM((cols * tokens, width), BF16),
            pltpu.VMEM((width, units), BF16),
            pltpu.VMEM((2 * tokens, units), F32),
            pltpu.VMEM((2, regs, width), F32),
            pltpu.VMEM((regs, width), F32),
            pltpu.VMEM((regs, width), F32),
            pltpu.VMEM((rows, regs, rw), F32),
            pltpu.VMEM((chips, regs, rw), F32),
            pltpu.VMEM((16, width), BF16),
            pltpu.VMEM((16, width), BF16),
            dma((5,)),
            dma((WPARTS,)),
            dma((CHUNKS, chips)),
            dma((CHUNKS, chips)),
            dma((CHUNKS, chips)),
            dma((CHUNKS, chips)),
            dma((GROUPS, 2)),
            dma((GROUPS, 2)),
            dma((GROUPS, 2)),
            dma((GROUPS, 2)),
            dma((2,)),
            dma((rows,)),
            dma((rows,)),
            dma((chips,)),
            dma((chips,)),
            dma((rows,)),
            dma((rows,)),
            dma((2,)),
        ],
        compiler_params=pltpu.CompilerParams(
            collective_id=0, has_side_effects=True, vmem_limit_bytes=VMEM_LIMIT
        ),
        name="block",
    )(
        flat(query_grid),
        flat(key_grid),
        flat(value_grid),
        flat(grad_output),
        flat(block_input),
        in_weight,
        sink_keys,
        sink_values,
        in_bias,
    )
    grid = jax.ShapeDtypeStruct((tokens, width), BF16)
    sink = jax.ShapeDtypeStruct((regs, width), BF16)
    out = pl.pallas_call(
        store,
        out_shape=(grid,) * 4 + (sink,) * 2 + (jax.ShapeDtypeStruct(shapes[5], BF16),),
        in_specs=[vmem] * 6,
        out_specs=(hbm,) * 7,
        scratch_shapes=[dma((7,))],
        compiler_params=pltpu.CompilerParams(vmem_limit_bytes=1024 * 1024),
        name="store",
    )(*(pltpu.with_memory_space_constraint(a, pltpu.VMEM) for a in held))
    shaped = tuple(a.reshape(tile_rows, tile_cols, width) for a in out[:4])
    return shaped + out[4:]


def solution(mesh):
    placed = (
        P("row", "col", None),
        P("row", "col", None),
        P("row", "col", None),
        P(),
        P(),
        P("row", "col", None),
        P("row", "col", None),
        P(None, "col"),
        P("col"),
    )
    return jax.shard_map(
        functools.partial(local, mesh.shape["row"], mesh.shape["col"]),
        mesh=mesh,
        in_specs=placed,
        out_specs=(
            P("row", "col", None),
            P("row", "col", None),
            P("row", "col", None),
            P("row", "col", None),
            P(),
            P(),
            P("row", None, "col"),
        ),
        check_vma=False,
    )
```

time: 113 us -> 84.1 us (0.74)
  Pallas kernels: 100 us -> 83.3 us
  local copies, waits for them, and re-layouts: 12.3 us -> 0 us
    pallas_call x1 -> x2, Pallas kernels: 100 us -> 83.3 us  [the longest x1 79.5 us: local(): pl.pallas_call(functools.partial(kernel, rows, cols), out_shape=tuple((pl...]
    unnamed x19 -> x0, local copies, waits for them, and re-layouts: 11 us -> none
    reshape x1 -> x0, local copies, waits for them, and re-layouts: 1.3 us -> none  [local(): in_bias.reshape(1, units)]
where the time goes in v1:
time: 84.1 us; the launch traced here: 83.9 us
  Pallas kernels  83.3 us (99%)
    pallas_call x1, Pallas kernels, local(): pl.pallas_call(functools.partial(kernel, rows, cols), out_shape=tuple((pl...  79.5 us
    pallas_call x1, Pallas kernels, local(): pl.pallas_call(store, out_shape=(grid,) * 4 + (sink,) * 2 + (jax.ShapeDty...  3.71 us

profile of v1, /device:TPU:0, one launch (start us, length us, event | category | flops | bytes accessed | tf_op | source)
XLA Modules:
  0.0 83.9 jit_solution(10440289370878454277)
XLA Ops:
  0.6 79.5 %block.1 = (bf16[128,6144]{1,0:T(8,128)(2,1)S(1)}, bf16[128,6144]{1,0:T(8,128)(2,1)S(1)}, bf16[128,6144]{1,0:T(8,128)(2,1)S(1)}, bf16[128,6144]{1,0:T(8,128)(2,1...) custom-call(bf16[128,6144]{1,0:T(8,128)(2,1)} %bitcast.9, bf16[128,6144]{1,0:T(8,128)(2,1)} %bitcast.10, ...), custom_call_target="tpu_custom_call" | custom-call | tf_op jit(solution)/shard_map/block/pallas_call | solution.py:633
  80.2 3.7 %store.1 = (bf16[128,6144]{1,0:T(8,128)(2,1)}, bf16[128,6144]{1,0:T(8,128)(2,1)}, bf16[128,6144]{1,0:T(8,128)(2,1)}, bf16[128,6144]{1,0:T(8,128)(2,1)}, bf16[8,6...) custom-call(bf16[128,6144]{1,0:T(8,128)(2,1)S(1)} %get-tuple-element.20.ao, ...), custom_call_target="tpu_custom_call" | custom-call | tf_op jit(solution)/shard_map/store/pallas_call | solution.py:686

commit v2 on v1

--- a/solution.py
+++ b/solution.py
@@ -15,9 +15,9 @@
 BF16 = jnp.bfloat16
 CHUNKS = 12
 GROUPS = 8
-UNROLL = 2
+UNROLL = 1
 NT = 512
-PIECES = 6
+EARLY = 2
 WPARTS = 6
 VMEM_LIMIT = 50 * 1024 * 1024
 
@@ -55,7 +55,7 @@
     w_in,
     sk_in,
     sv_in,
-    bias,
+    bias_in,
     gb,
     qb,
     kb,
@@ -76,6 +76,7 @@
     rc,
     sk,
     sv,
+    bias,
     load_sem,
     w_sem,
     xs_sem,
@@ -107,10 +108,10 @@
     gw = width // GROUPS
     rw = width // rows
     wk = width // WPARTS
-    pw = width // PIECES
+    pw = 2 * kc
     pair = 2 * tokens
     scale = 1.0 / math.sqrt(HEAD_DIM)
-    nt = min(NT, units)
+    nt = NT if units % NT == 0 else NT // 2
     n_tiles = units // nt
 
     my_row = lax.axis_index("row")
@@ -136,12 +137,6 @@
 
     def load(src, dst, s):
         return pltpu.make_async_copy(src, dst, load_sem.at[s])
-
-    own_rows = pl.ds(pl.multiple_of(my_col * tokens, tokens), tokens)
-    grads = ((q_in, qb), (k_in, kb), (v_in, vb), (g_in, gb))
-    load(x_in, xg.at[own_rows, :], 4).start()
-    for s, (src, dst) in enumerate(grads):
-        load(src, dst, s).start()
 
     barrier = pltpu.get_barrier_semaphore()
     pl.semaphore_signal(barrier, inc=1, device_id=peer, device_id_type=MESH)
@@ -150,9 +145,23 @@
     for d in range(1, rows):
         pl.semaphore_signal(barrier, inc=1, device_id=row_dev(d), device_id_type=MESH)
 
-    for pad, given in ((sk, sk_in), (sv, sv_in)):
-        pad[...] = jnp.zeros_like(pad)
-        pad[:regs, :] = given[...]
+    own_rows = pl.ds(pl.multiple_of(my_col * tokens, tokens), tokens)
+    loads = (
+        (q_in, qb),
+        (k_in, kb),
+        (v_in, vb),
+        (g_in, gb),
+        (sk_in, sk.at[:regs, :]),
+        (sv_in, sv.at[:regs, :]),
+        (bias_in, bias),
+        (x_in, xg.at[own_rows, :]),
+    )
+    own = len(loads) - 1
+    for pad in (sk, sv):
+        pad[regs:, :] = jnp.zeros((pad.shape[0] - regs, width), BF16)
+
+    for s in range(own):
+        load(*loads[s], s).start()
 
     pl.semaphore_wait(barrier, 1 + chips - 1 + rows - 1)
 
@@ -190,10 +199,13 @@
             pl.ds(pl.multiple_of(c * kc, kc), kc),
         ]
 
+    def mine(c):
+        return x_in.at[:, pl.ds(pl.multiple_of(c * kc, kc), kc)]
+
     def hop(c, r, up):
         block = piece(c, up, parity)
         return pltpu.make_async_remote_copy(
-            src_ref=block,
+            src_ref=block if up else mine(c),
             dst_ref=block,
             send_sem=xs_sem.at[c, r],
             recv_sem=xr_sem.at[c, r],
@@ -215,7 +227,7 @@
     def share(c, r):
         block = piece(c, r, parity)
         return pltpu.make_async_remote_copy(
-            src_ref=block,
+            src_ref=block if r else mine(c),
             dst_ref=block,
             send_sem=ps_sem.at[c, r],
             recv_sem=pr_sem.at[c, r],
@@ -263,7 +275,6 @@
 
     for which in range(2):
         kv_copy(0, which).start()
-    load(x_in, xg.at[own_rows, :], 4).wait()
     for leaf in range(2):
 
         @pl.loop(0, half)
@@ -282,51 +293,68 @@
     def _(c):
         share(c, 0).start()
 
+    load(*loads[own], own).start()
+
     @pl.loop(0, WPARTS)
     def _(c):
         w_copy(c).start()
 
-    for s, (src, dst) in enumerate(grads):
-        load(src, dst, s).wait()
-
-    lane = lax.broadcasted_iota(jnp.int32, (tokens, HEAD_DIM), 1)
+    for s in range(own):
+        load(*loads[s], s).wait()
+
+    n_keys = pair + regs
+    fill = sk.shape[0] - regs
+    to_log2 = scale * math.log2(math.e)
+
+    def diagonal(a):
+        blank = jnp.zeros((tokens, HEAD_DIM), BF16)
+        return jnp.concatenate(
+            [
+                jnp.concatenate([a[:, :HEAD_DIM], blank], axis=1),
+                jnp.concatenate([blank, a[:, HEAD_DIM:]], axis=1),
+            ],
+            axis=0,
+        )
+
+    def padded(a):
+        return jnp.concatenate([a, jnp.zeros((fill, a.shape[1]), F32)], axis=0).astype(BF16)
 
     def attend(first):
         at = [
-            pl.ds(pl.multiple_of((first + j) * HEAD_DIM, HEAD_DIM), HEAD_DIM)
+            pl.ds(pl.multiple_of((first + 2 * j) * HEAD_DIM, 2 * HEAD_DIM), 2 * HEAD_DIM)
             for j in range(UNROLL)
         ]
-        blank = jnp.zeros((HEAD_DIM - sk.shape[0], HEAD_DIM), BF16)
         done = []
         for c in at:
-            q = qb[:, c]
-            g = gb[:, c]
-            keys = jnp.concatenate([kb[:, c], pk[:, c], sk[:, c], blank], axis=0)
-            values = jnp.concatenate([vb[:, c], pv[:, c], sv[:, c], blank], axis=0)
-            s = dot_nt(q, keys) * scale
-            sw = s[:, : 2 * tokens]
-            ss = jnp.where(lane < regs, s[:, 2 * tokens :], -1e30)
-            s = jnp.concatenate([sw, ss], axis=1)
-            e = jnp.exp(s - jnp.max(s, axis=-1, keepdims=True))
-            p = e * (1.0 / jnp.sum(e, axis=-1, keepdims=True))
-            weight = p.astype(BF16)
-            o = dot_nn(weight, values).astype(BF16)
-            delta = jnp.sum(g.astype(F32) * o.astype(F32), axis=-1, keepdims=True)
-            dp = dot_nt(g, values)
-            ds = (p * (dp - delta) * scale).astype(BF16)
-            dq = dot_nn(ds, keys).astype(BF16)
-            dk = dot_tn(ds, q)
-            dv = dot_tn(weight, g)
+            keys = jnp.concatenate([kb[:, c], pk[:, c], sk[:, c]], axis=0)
+            values = jnp.concatenate([vb[:, c], pv[:, c], sv[:, c]], axis=0)
+            qd = diagonal(qb[:, c])
+            gd = diagonal(gb[:, c])
+            s = dot_nt(keys, qd)[:n_keys] * to_log2
+            dp = dot_nt(values, gd)[:n_keys]
+            e = jnp.exp2(s - jnp.max(s, axis=0, keepdims=True))
+            inv = 1.0 / jnp.sum(e, axis=0, keepdims=True)
+            delta = jnp.sum(e * dp, axis=0, keepdims=True) * inv
+            weight = padded(e * inv)
+            ds = padded((e * (inv * scale)) * (dp - delta))
+            dv = dot_nn(weight, gd)
+            dk = dot_nn(ds, qd)
+            o = []
+            dq = []
+            for h in range(2):
+                at_h = slice(h * HEAD_DIM, (h + 1) * HEAD_DIM)
+                o.append(dot_tn(weight[:, at_h], values[:, at_h]))
+                dq.append(dot_tn(ds[:, at_h], keys[:, at_h]))
             done.append((o, dq, dk, dv))
         for c, (o, dq, dk, dv) in zip(at, done):
-            gb[:, c] = o
-            qb[:, c] = dq
+            gb[:, c] = jnp.concatenate(o, axis=1).astype(BF16)
+            qb[:, c] = jnp.concatenate(dq, axis=1).astype(BF16)
             kb[:, c] = dk[:tokens].astype(BF16)
-            pk[:, c] = dk[tokens : 2 * tokens].astype(BF16)
+            pk[:, c] = dk[tokens:pair].astype(BF16)
             vb[:, c] = dv[:tokens].astype(BF16)
-            pv[:, c] = dv[tokens : 2 * tokens].astype(BF16)
-            sg[0, :, c] = dk[2 * tokens : 2 * tokens + regs]
-            sg[1, :, c] = dv[2 * tokens : 2 * tokens + regs]
+            pv[:, c] = dv[tokens:pair].astype(BF16)
+            sg[0, :, c] = dk[pair:n_keys]
+            sg[1, :, c] = dv[pair:n_keys]
 
     def rows_of(r):
         return pl.ds(pl.multiple_of(flipped(chip, r) * pair, pair), pair)
@@ -421,16 +449,16 @@
         for d in range(1, rows):
             b_copy(d).wait_recv()
             total = total + rb[d]
-        rc[chip] = total
+        rc[chip] = total.astype(BF16)
         for r in range(1, chips):
             c_copy(r, chip).start()
 
     def sinks_d():
         for r in range(1, chips):
             c_copy(r, flipped(chip, r)).wait_recv()
-        total = rc[0]
+        total = rc[0].astype(F32)
         for r in range(1, chips):
-            total = total + rc[r]
+            total = total + rc[r].astype(F32)
         fin[parity, :, row_cols(my_row)] = total.astype(BF16)
         for d in range(1, rows):
             d_copy(d, my_row).start()
@@ -447,9 +475,9 @@
             for which in range(2):
                 kv_copy(i, which).wait_recv()
 
-            @pl.loop(0, per_group // UNROLL)
+            @pl.loop(0, per_group // (2 * UNROLL))
             def _(j):
-                attend(i * per_group + j * UNROLL)
+                attend(i * per_group + j * 2 * UNROLL)
 
             for which in range(2):
                 grad_copy(i, which).start()
@@ -458,15 +486,17 @@
         def _():
             finish_group(i - 1)
 
-        @pl.when(i < half)
-        def _():
-            forward(i)
-
-        @pl.when(i >= half)
-        def _():
-            settle(i - half)
+        for j in range(EARLY):
+
+            @pl.when(i == GROUPS - 2 * (EARLY - j))
+            def _():
+                forward(j)
 
     a_copy().start()
+    for n in range(n_tiles):
+        ncols = tile_cols(n)
+        acc[:, ncols] = jnp.broadcast_to(bias[ncols], (last * pair, nt))
+    load(*loads[own], own).wait()
 
     @pl.loop(0, WPARTS)
     def _(c):
@@ -476,8 +506,6 @@
     def _(c):
         share_in(c, 0).wait_recv()
 
-    done = GROUPS + 1 - half
-
     @pl.loop(0, n_tiles)
     def _(n):
         whole_rows(0, n)
@@ -486,74 +514,61 @@
         def _():
             sinks_b()
 
-        @pl.when(n + done < half)
+        @pl.when(n == n_tiles - 1)
         def _():
-            settle(n + done)
-
-    @pl.loop(min(half, n_tiles + done), half)
+            sinks_c()
+
+    @pl.loop(EARLY, half)
     def _(j):
-        settle(j)
-
-    sinks_c()
-
-    for level in range(2, levels):
-
-        @pl.loop(0, half)
+        forward(j)
+
+    def sum_rows(r):
+        return slice((r - 1) * pair, r * pair)
+
+    def mix(j, r):
+        kcols = pl.ds(pl.multiple_of(j * pw, pw), pw)
+        x = xg[rows_of(r), kcols]
+        for n in range(n_tiles):
+            ncols = tile_cols(n)
+            acc[sum_rows(r), ncols] += dot_nn(x, wv[kcols, ncols])
+
+    for level in range(1, levels + 1):
+        here = [r for r in range(1, chips) if bits(r) == level]
+
+        @pl.loop(0, half + 1)
         def _(j):
-            for r in range(1, chips):
-                if bits(r) == level:
+            @pl.when(j < half)
+            def _():
+                if level == 1:
+                    settle(j)
+                else:
+                    for r in here:
+                        for tree in range(2):
+                            pass_on(j, r, tree)
+
+            @pl.when(j >= 1)
+            def _():
+                for r in here:
                     for tree in range(2):
-                        pass_on(j, r, tree)
-
-    for r in sorted(range(1, last), key=bits):
-
-        @pl.loop(0, CHUNKS)
-        def _(c):
-            share_in(c, r).wait_recv()
-
-        @pl.loop(0, n_tiles)
-        def _(n):
-            whole_rows(r, n)
-
-    def take(j):
-        for c in range(CHUNKS // PIECES):
-            c = j * (CHUNKS // PIECES) + c
-            hop_in(c, last).wait_recv()
-            share(c, last).start()
-
-    def mix(j, n, part):
-        kcols = pl.ds(pl.multiple_of(j * pw, pw), pw)
-        ncols = tile_cols(n)
-        z = dot_nn(xg[rows_of(last), kcols], wv[kcols, ncols])
-        if part == 0:
-            acc[:, ncols] = z + bias[ncols]
-        elif part == 1:
-            acc[:, ncols] += z
-        else:
-            finish(acc[:, ncols] + z, last, ncols)
-
-    take(0)
-    take(1)
-    for part, (lo, hi) in enumerate(((0, 1), (1, PIECES - 1), (PIECES - 1, PIECES))):
-
-        @pl.loop(lo, hi)
-        def _(j):
-            for c in range(CHUNKS // PIECES):
-                share_in(j * (CHUNKS // PIECES) + c, last).wait_recv()
+                        share_in(2 * (j - 1) + tree, r).wait_recv()
+                    mix(j - 1, r)
+
+            if level == levels:
+
+                @pl.when(j == half - 3)
+                def _():
+                    sinks_d()
+
+                @pl.when(j == half - 1)
+                def _():
+                    sinks_e()
+
+        for r in here:
 
             @pl.loop(0, n_tiles)
             def _(n):
-                mix(j, n, part)
-
-            @pl.when(j + 2 < PIECES)
-            def _():
-                take(j + 2)
-
-            @pl.when(j == PIECES - 2)
-            def _():
-                sinks_d()
-
-    sinks_e()
+                ncols = tile_cols(n)
+                finish(acc[sum_rows(r), ncols], r, ncols)
 
     @pl.loop(0, CHUNKS)
     def _(c):
@@ -633,21 +648,22 @@
     held = pl.pallas_call(
         functools.partial(kernel, rows, cols),
         out_shape=tuple(pltpu.VMEM(shape, BF16) for shape in shapes),
-        in_specs=[hbm] * 6 + [vmem] * 3,
+        in_specs=[hbm] * 9,
         out_specs=(vmem,) * 6,
         scratch_shapes=[block] * 4
         + [
             pltpu.VMEM((cols * tokens, width), BF16),
             pltpu.VMEM((width, units), BF16),
-            pltpu.VMEM((2 * tokens, units), F32),
+            pltpu.VMEM(((chips - 1) * 2 * tokens, units), F32),
             pltpu.VMEM((2, regs, width), F32),
             pltpu.VMEM((regs, width), F32),
             pltpu.VMEM((regs, width), F32),
             pltpu.VMEM((rows, regs, rw), F32),
-            pltpu.VMEM((chips, regs, rw), F32),
+            pltpu.VMEM((chips, regs, rw), BF16),
             pltpu.VMEM((16, width), BF16),
             pltpu.VMEM((16, width), BF16),
-            dma((5,)),
+            pltpu.VMEM((units,), F32),
+            dma((8,)),
             dma((WPARTS,)),
             dma((CHUNKS, chips)),
             dma((CHUNKS, chips)),

time: 84.1 us -> 69 us (0.82)
  Pallas kernels: 83.3 us -> 68.2 us
    pallas_call x1, Pallas kernels: 79.5 us -> 64.5 us  [local(): pl.pallas_call(functools.partial(kernel, rows, cols), out_shape=tuple((pl...]
where the time goes in v2:
time: 69 us; the launch traced here: 68.8 us
  Pallas kernels  68.2 us (99%)
    pallas_call x1, Pallas kernels, local(): pl.pallas_call(functools.partial(kernel, rows, cols), out_shape=tuple((pl...  64.5 us
    pallas_call x1, Pallas kernels, local(): pl.pallas_call(store, out_shape=(grid,) * 4 + (sink,) * 2 + (jax.ShapeDty...  3.71 us

profile of v2, /device:TPU:0, one launch (start us, length us, event | category | flops | bytes accessed | tf_op | source)
XLA Modules:
  0.0 68.8 jit_solution(5919427963833861795)
XLA Ops:
  0.6 64.5 %block.1 = (bf16[128,6144]{1,0:T(8,128)(2,1)S(1)}, bf16[128,6144]{1,0:T(8,128)(2,1)S(1)}, bf16[128,6144]{1,0:T(8,128)(2,1)S(1)}, bf16[128,6144]{1,0:T(8,128)(2,1...) custom-call(bf16[128,6144]{1,0:T(8,128)(2,1)} %bitcast.9, bf16[128,6144]{1,0:T(8,128)(2,1)} %bitcast.10, ...), custom_call_target="tpu_custom_call" | custom-call | tf_op jit(solution)/shard_map/block/pallas_call | solution.py:648
  65.1 3.7 %store.1 = (bf16[128,6144]{1,0:T(8,128)(2,1)}, bf16[128,6144]{1,0:T(8,128)(2,1)}, bf16[128,6144]{1,0:T(8,128)(2,1)}, bf16[128,6144]{1,0:T(8,128)(2,1)}, bf16[8,6...) custom-call(bf16[128,6144]{1,0:T(8,128)(2,1)S(1)} %get-tuple-element.20.ao, ...), custom_call_target="tpu_custom_call" | custom-call | tf_op jit(solution)/shard_map/store/pallas_call | solution.py:702
